TPU v7x, 32 devices: a whole 2x2x4 slice. The times are simulated.
32 devices in a mesh: row: 8 (over z, x), col: 4 (over y, core).
Axes of the slice: x: 2, y: 2, z: 4, core: 2. Of those that a mesh axis runs over, the one named last changes fastest.
Arguments:
- trailing: float32 [16384, 8192], P('row', 'col'), may hold values from -6 to 6
- vectors: float32 [16384, 256], P(('row', 'col')), may hold values from -0.1875 to 0.1875
- tfactor: float32 [256, 256], replicated, may hold values from -0.375 to 0.375
Outputs:
- updated: float32 [16384, 8192], P('row', 'col')
All inputs are finite; a program needn't handle non-finite values.
Results may differ from a plain program's by a relative error of at most 0.0003.
Values sent between devices are 32-bit elements.
A program may use at most 128 MiB of HBM per device.

v0:
```python
import jax
import jax.numpy as jnp
from jax import lax
from jax.sharding import PartitionSpec as P


def shards(trailing, vectors, tfactor):
    high = lax.Precision.HIGHEST
    near_vectors = lax.all_gather(vectors, "col", axis=0, tiled=True)
    partial_value = jnp.dot(
        near_vectors.T, trailing, precision=high, preferred_element_type=jnp.float32
    )
    summed = lax.psum(partial_value, "row")
    scaled = jnp.dot(tfactor, summed, precision=high, preferred_element_type=jnp.float32)
    change = jnp.dot(near_vectors, scaled, precision=high, preferred_element_type=jnp.float32)
    return trailing - change


def solution(mesh):
    placed = (P("row", "col"), P(("row", "col"), None), P())
    return jax.shard_map(
        shards, mesh=mesh, in_specs=placed, out_specs=P("row", "col"), check_vma=False
    )
```

profile of v0, /device:TPU:0, one launch (start us, length us, event | category | flops | bytes accessed | tf_op | source)
XLA Modules:
  0.0 203.2 jit_solution(18051398769543396435)
XLA Ops:
  6.5 0.0 copy-start
  6.5 0.0 all-gather.2.cloned.1.call-start
  6.5 0.7 all-gather.2.cloned.1.call-update
  7.3 0.0 all-reduce.2.cloned.1.call-start
  7.3 26.9 %all-gather.2.cloned.1.call-done = f32[2048,256]{1,0:T(8,128)} async-done(((f32[512,256]{1,0:T(8,128)}), f32[2048,256]{1,0:T(8,128)}) %all-gather.2.cloned.1.call-update) | async-done | bytes 2097168 | tf_op jit(solution)/shard_map/all_gather | solution.py:9
  34.2 18.3 %fusion = f32[256,2048]{1,0:T(8,128)} fusion(f32[2048,256]{1,0:T(8,128)} %all-gather.2.cloned.1.call-done, f32[2048,2048]{1,0:T(8,128)} %param.3), kind=kOutput, calls=%fused_computation.1 | convolution fusion | flops 12884901888 | bytes 20971520 | tf_op jit(solution)/shard_map/dot_general | solution.py:10
  52.5 0.0 all-reduce.2.cloned.1.call-update
  52.5 17.7 %copy.4 = f32[2048,2048]{0,1:T(8,128)} copy(f32[2048,2048]{1,0:T(8,128)} %param.3) | data formatting | bytes 33554432 | tf_op args[0]
  70.2 0.0 copy-start.2
  70.2 84.8 %all-reduce.2.cloned.1.call-done = f32[256,2048]{1,0:T(8,128)} async-done(((f32[256,2048]{1,0:T(8,128)}), f32[256,2048]{1,0:T(8,128)}) %all-reduce.2.cloned.1.call-update) | async-done | bytes 2097168 | tf_op jit(solution)/shard_map/psum | solution.py:13
  155.0 0.0 copy-done
  155.0 5.2 %fusion.1 = f32[2048,256]{1,0:T(8,128)S(1)} fusion(f32[256,2048]{1,0:T(8,128)} %all-reduce.2.cloned.1.call-done, f32[256,256]{1,0:T(8,128)S(1)} %copy-done), kind=kOutput, calls=%fused_computation.2 | convolution fusion | flops 1610612736 | bytes 4456448 | tf_op jit(solution)/shard_map/dot_general | solution.py:14
  160.2 0.0 copy-done.2
  160.2 18.5 %bitcast_subtract_fusion = f32[2048,2048]{0,1:T(8,128)} fusion(f32[2048,2048]{0,1:T(8,128)} %copy.4, f32[2048,256]{1,0:T(8,128)S(1)} %fusion.1, f32[2048,256]{1,0:T(8,128)S(1)} %copy-done.2), kind=kOutput, calls=%fused_computation | convolution fusion | flops 12889096192 | bytes 37748736 | tf_op jit(solution)/shard_map/dot_general | solution.py:15
  178.7 0.0 copy-start.1
  178.7 17.6 %copy.5 = f32[2048,2048]{1,0:T(8,128)} copy(f32[2048,2048]{0,1:T(8,128)} %bitcast_subtract_fusion) | data formatting | bytes 33554432 | tf_op jit(solution)/shard_map/sub | solution.py:16
  196.3 0.0 copy-done.1
Async XLA Ops:
  6.5 148.5 %copy-start = (f32[256,256]{1,0:T(8,128)S(1)}, f32[256,256]{1,0:T(8,128)}, u32[]{:S(2)}) copy-start(f32[256,256]{1,0:T(8,128)} %param.5) | copy-start | bytes 786436
  6.5 27.7 %all-gather.2.cloned.1.call-start = ((), (), s32[]{:S(2)}) async-start(), calls=%async_computation | async-start | bytes 2621440 | tf_op jit(solution)/shard_map/all_gather | solution.py:9
  7.3 147.7 %all-reduce.2.cloned.1.call-start = ((), (), s32[]{:S(2)}) async-start(), calls=%async_computation.1 | async-start | bytes 4194304 | tf_op jit(solution)/shard_map/psum | solution.py:13
  70.2 90.0 %copy-start.2 = (f32[2048,256]{1,0:T(8,128)S(1)}, f32[2048,256]{1,0:T(8,128)}, u32[]{:S(2)}) copy-start(f32[2048,256]{1,0:T(8,128)} %all-gather.2.cloned.1.call-done) | copy-start | bytes 6291460
  178.7 17.6 %copy-start.1 = (f32[256,256]{1,0:T(8,128)S(1)}, f32[256,256]{1,0:T(8,128)}, u32[]{:S(2)}) copy-start(f32[256,256]{1,0:T(8,128)} %param.5) | copy-start | bytes 786436
Sparse Core Ops, SparseCore 0:
  8.9 25.2 all-gather.1
  52.7 102.2 all-reduce.1
where the time goes:
time: 204 us; the launch traced here: 203 us
  waiting for transfers between devices  112 us (55%)
  matrix products  42 us (21%)
  local copies, waits for them, and re-layouts  35.3 us (17%)
  between operations  13.4 us (7%)
    psum x1, waiting for transfers between devices, shards(): summed = lax.psum(partial_value, 'row')  84.8 us
    all_gather x1, waiting for transfers between devices, shards(): near_vectors = lax.all_gather(vectors, 'col', axis=0, tiled=True)  26.9 us
    dot_general x1, matrix products, shards(): jnp.dot(near_vectors, scaled, precision=high, preferred_element_type=jnp....  18.5 us
    dot_general x1, matrix products, shards(): jnp.dot(near_vectors.T, trailing, precision=high, preferred_element_type=...  18.3 us
    unnamed x7, local copies, waits for them, and re-layouts  17.7 us
    sub x1, local copies, waits for them, and re-layouts, shards(): return trailing - change  17.6 us
    dot_general x1, matrix products, shards(): jnp.dot(tfactor, summed, precision=high, preferred_element_type=jnp.float32)  5.17 us
  transfers between devices with their start and end apart: 2, of which 2 were waited for; matrix products, arithmetic and copies ran while one was open for 9% of the time, Pallas kernels for 0%

commit v1 on v0

--- a/solution.py
+++ b/solution.py
@@ -10,7 +10,7 @@
     partial_value = jnp.dot(
         near_vectors.T, trailing, precision=high, preferred_element_type=jnp.float32
     )
-    summed = lax.psum(partial_value, "row")
+    summed = jnp.sum(lax.all_gather(partial_value, "row"), axis=0)
     scaled = jnp.dot(tfactor, summed, precision=high, preferred_element_type=jnp.float32)
     change = jnp.dot(near_vectors, scaled, precision=high, preferred_element_type=jnp.float32)
     return trailing - change

time: 204 us -> 335 us (1.64)
  waiting for transfers between devices: 112 us -> 237 us
  other arithmetic: 0 us -> 7.76 us
    all_gather x0 -> x1, waiting for transfers between devices: none -> 209 us  [shards(): summed = jnp.sum(lax.all_gather(partial_value, 'row'), axis=0)]
    psum x1 -> x0, waiting for transfers between devices: 84.8 us -> none  [shards(): summed = lax.psum(partial_value, 'row')]
    reduce_sum x0 -> x1, other arithmetic: none -> 7.76 us  [shards(): summed = jnp.sum(lax.all_gather(partial_value, 'row'), axis=0)]
  transfers between devices with their start and end apart: 2 -> 2, of which waited for: 2 -> 2; matrix products, arithmetic and copies ran while one was open for 9% -> 5% of each run, Pallas kernels for 0% -> 0%
where the time goes in v1:
time: 335 us; the launch traced here: 334 us
  waiting for transfers between devices  237 us (71%)
  matrix products  40.5 us (12%)
  local copies, waits for them, and re-layouts  35.6 us (11%)
  between operations  13.4 us (4%)
  other arithmetic  7.76 us (2%)
    all_gather x1, waiting for transfers between devices, shards(): summed = jnp.sum(lax.all_gather(partial_value, 'row'), axis=0)  209 us
    all_gather x1, waiting for transfers between devices, shards(): near_vectors = lax.all_gather(vectors, 'col', axis=0, tiled=True)  26.9 us
    dot_general x1, matrix products, shards(): jnp.dot(near_vectors, scaled, precision=high, preferred_element_type=jnp....  18.7 us
    dot_general x1, matrix products, shards(): jnp.dot(near_vectors.T, trailing, precision=high, preferred_element_type=...  18.3 us
    unnamed x7, local copies, waits for them, and re-layouts  18 us
    sub x1, local copies, waits for them, and re-layouts, shards(): return trailing - change  17.6 us
    reduce_sum x1, other arithmetic, shards(): summed = jnp.sum(lax.all_gather(partial_value, 'row'), axis=0)  7.76 us
  transfers between devices with their start and end apart: 2, of which 2 were waited for; matrix products, arithmetic and copies ran while one was open for 5% of the time, Pallas kernels for 0%

profile of v1, /device:TPU:0, one launch (start us, length us, event | category | flops | bytes accessed | tf_op | source)
XLA Modules:
  0.0 334.5 jit_solution(3366589063080867662)
XLA Ops:
  6.5 0.0 copy-start
  6.5 0.0 all-gather.4.cloned.1.call-start
  6.5 0.7 all-gather.4.cloned.1.call-update
  7.3 0.0 all-gather.6.cloned.1.call-start
  7.3 26.9 %all-gather.4.cloned.1.call-done = f32[2048,256]{1,0:T(8,128)} async-done(((f32[512,256]{1,0:T(8,128)}), f32[2048,256]{1,0:T(8,128)}) %all-gather.4.cloned.1.call-update) | async-done | bytes 2097168 | tf_op jit(solution)/shard_map/all_gather | solution.py:9
  34.2 18.3 %fusion = f32[256,2048]{1,0:T(8,128)} fusion(f32[2048,256]{1,0:T(8,128)} %all-gather.4.cloned.1.call-done, f32[2048,2048]{1,0:T(8,128)} %param.3), kind=kOutput, calls=%fused_computation.1 | convolution fusion | flops 12884901888 | bytes 20971520 | tf_op jit(solution)/shard_map/dot_general | solution.py:10
  52.5 0.0 all-gather.6.cloned.1.call-update
  52.6 18.0 %copy.4 = f32[2048,2048]{0,1:T(8,128)} copy(f32[2048,2048]{1,0:T(8,128)} %param.3) | data formatting | bytes 33554432 | tf_op args[0]
  70.5 209.5 %all-gather.6.cloned.1.call-done = f32[2048,2048]{1,0:T(8,128)} async-done(((f32[256,2048]{1,0:T(8,128)}), f32[2048,2048]{1,0:T(8,128)}) %all-gather.6.cloned.1.call-update) | async-done | bytes 16777232 | tf_op jit(solution)/shard_map/all_gather | solution.py:13
  280.0 7.8 %reduce_sum.9 = f32[256,2048]{1,0:T(8,128)S(1)} reduce(f32[8,256,2048]{2,1,0:T(8,128)} %bitcast.9, f32[]{:T(128)} %constant.0.clone.1), dimensions={0}, to_apply=%region_0.0 | reduce | flops 3670016 | bytes 18874372 | tf_op jit(solution)/shard_map/reduce_sum | solution.py:13
  287.8 0.0 copy-done
  287.8 0.0 copy-start.2
  287.8 3.5 %fusion.1 = f32[2048,256]{1,0:T(8,128)S(1)} fusion(f32[256,2048]{1,0:T(8,128)S(1)} %reduce_sum.9, f32[256,256]{1,0:T(8,128)S(1)} %copy-done), kind=kOutput, calls=%fused_computation.2 | convolution fusion | flops 1610612736 | bytes 4456448 | tf_op jit(solution)/shard_map/dot_general | solution.py:14
  291.3 0.0 copy-done.2
  291.3 18.7 %bitcast_subtract_fusion = f32[2048,2048]{0,1:T(8,128)} fusion(f32[2048,2048]{0,1:T(8,128)} %copy.4, f32[2048,256]{1,0:T(8,128)S(1)} %fusion.1, f32[2048,256]{1,0:T(8,128)S(1)} %copy-done.2), kind=kOutput, calls=%fused_computation | convolution fusion | flops 12889096192 | bytes 37748736 | tf_op jit(solution)/shard_map/dot_general | solution.py:15
  310.0 0.0 copy-start.1
  310.0 17.6 %copy.5 = f32[2048,2048]{1,0:T(8,128)} copy(f32[2048,2048]{0,1:T(8,128)} %bitcast_subtract_fusion) | data formatting | bytes 33554432 | tf_op jit(solution)/shard_map/sub | solution.py:16
  327.6 0.0 copy-done.1
Async XLA Ops:
  6.5 281.2 %copy-start = (f32[256,256]{1,0:T(8,128)S(1)}, f32[256,256]{1,0:T(8,128)}, u32[]{:S(2)}) copy-start(f32[256,256]{1,0:T(8,128)} %param.5) | copy-start | bytes 786436
  6.5 27.7 %all-gather.4.cloned.1.call-start = ((), (), s32[]{:S(2)}) async-start(), calls=%async_computation | async-start | bytes 2621440 | tf_op jit(solution)/shard_map/all_gather | solution.py:9
  7.3 272.7 %all-gather.6.cloned.1.call-start = ((), (), s32[]{:S(2)}) async-start(), calls=%async_computation.1 | async-start | bytes 18874368 | tf_op jit(solution)/shard_map/all_gather | solution.py:13
  287.8 3.5 %copy-start.2 = (f32[2048,256]{1,0:T(8,128)S(1)}, f32[2048,256]{1,0:T(8,128)}, u32[]{:S(2)}) copy-start(f32[2048,256]{1,0:T(8,128)} %all-gather.4.cloned.1.call-done) | copy-start | bytes 6291460
  310.0 17.6 %copy-start.1 = (f32[256,256]{1,0:T(8,128)S(1)}, f32[256,256]{1,0:T(8,128)}, u32[]{:S(2)}) copy-start(f32[256,256]{1,0:T(8,128)} %param.5) | copy-start | bytes 786436
Sparse Core Ops, SparseCore 0:
  8.9 25.2 all-gather.3
  52.7 227.2 all-gather.5

commit v2 on v0

--- a/solution.py
+++ b/solution.py
@@ -6,7 +6,12 @@
 
 def shards(trailing, vectors, tfactor):
     high = lax.Precision.HIGHEST
-    near_vectors = lax.all_gather(vectors, "col", axis=0, tiled=True)
+    ring = [vectors]
+    for hop in range(3):
+        ring.append(lax.ppermute(ring[-1], "col", [(dev, (dev + 1) % 4) for dev in range(4)]))
+    near_vectors = jnp.roll(
+        jnp.concatenate(ring[::-1], axis=0), (lax.axis_index("col") + 1) * ring[0].shape[0], axis=0
+    )
     partial_value = jnp.dot(
         near_vectors.T, trailing, precision=high, preferred_element_type=jnp.float32
     )

time: 204 us -> 190 us (0.931)
  local copies, waits for them, and re-layouts: 35.3 us -> 3.35 us
  waiting for transfers between devices: 112 us -> 131 us
    all_gather x1 -> x0, waiting for transfers between devices: 26.9 us -> none  [shards(): near_vectors = lax.all_gather(vectors, 'col', axis=0, tiled=True)]
    ppermute x0 -> x3, waiting for transfers between devices: none -> 26.2 us  [shards(): lax.ppermute(ring[-1], 'col', [(dev, (dev + 1) % 4) for dev in range(4)])]
    psum x1, waiting for transfers between devices: 84.8 us -> 104 us  [shards(): summed = lax.psum(partial_value, 'row')]
    sub x1 -> x0, local copies, waits for them, and re-layouts: 17.6 us -> none  [shards(): return trailing - change]
    unnamed x7 -> x15, local copies, waits for them, and re-layouts: 17.7 us -> 3.32 us
  transfers between devices with their start and end apart: 2 -> 4, of which waited for: 2 -> 4; matrix products, arithmetic and copies ran while one was open for 9% -> 0% of each run, Pallas kernels for 0% -> 0%
where the time goes in v2:
time: 190 us
  waiting for transfers between devices  131 us (69%)
  matrix products  41.5 us (22%)
  between operations  13.5 us (7%)
  local copies, waits for them, and re-layouts  3.35 us (2%)
    psum x1, waiting for transfers between devices, shards(): summed = lax.psum(partial_value, 'row')  104 us
    ppermute x3, waiting for transfers between devices, shards(): lax.ppermute(ring[-1], 'col', [(dev, (dev + 1) % 4) for dev in range(4)])  26.2 us
    dot_general x1, matrix products, shards(): jnp.dot(near_vectors, scaled, precision=high, preferred_element_type=jnp....  18.5 us
    dot_general x1, matrix products, shards(): jnp.dot(near_vectors.T, trailing, precision=high, preferred_element_type=...  17.7 us
    dot_general x1, matrix products, shards(): jnp.dot(tfactor, summed, precision=high, preferred_element_type=jnp.float32)  5.32 us
  transfers between devices with their start and end apart: 4, of which 4 were waited for; matrix products, arithmetic and copies ran while one was open for 0% of the time, Pallas kernels for 0%

profile of v2, /device:TPU:0, one launch (start us, length us, event | category | flops | bytes accessed | tf_op | source)
XLA Modules:
  0.0 189.6 jit_solution(16563419707419132213)
XLA Ops:
  6.5 0.0 copy-start
  6.5 0.0 copy-start.3
  6.5 0.0 all-reduce.2.cloned.1.call-start
  6.5 0.5 collective-permute-start
  7.0 9.0 %collective-permute-done = f32[512,256]{1,0:T(8,128)S(1)} collective-permute-done((f32[512,256]{1,0:T(8,128)}, f32[512,256]{1,0:T(8,128)S(1)}, u32[]{:S(2)}, u32[]{:S(2)}) %collective-permute-start) | collective-permute-done | bytes 524320 | tf_op jit(solution)/shard_map/ppermute | solution.py:11
  16.1 0.0 collective-permute-start.1
  16.1 8.6 %collective-permute-done.1 = f32[512,256]{1,0:T(8,128)S(1)} collective-permute-done((f32[512,256]{1,0:T(8,128)S(1)}, f32[512,256]{1,0:T(8,128)S(1)}, u32[]{:S(2)}, u32[]{:S(2)}) %collective-permute-start.1) | collective-permute-done | bytes 524320 | tf_op jit(solution)/shard_map/ppermute | solution.py:11
  24.7 0.0 collective-permute-start.2
  24.7 8.6 %collective-permute-done.2 = f32[512,256]{1,0:T(8,128)S(1)} collective-permute-done((f32[512,256]{1,0:T(8,128)S(1)}, f32[512,256]{1,0:T(8,128)S(1)}, u32[]{:S(2)}, u32[]{:S(2)}) %collective-permute-start.2) | collective-permute-done | bytes 524320 | tf_op jit(solution)/shard_map/ppermute | solution.py:11
  33.4 1.1 constant_dynamic-update-slice_fusion.4
  34.6 0.0 copy-done.3
  34.7 0.0 copy-start.1
  34.7 2.0 %copy-done.1 = f32[4096,256]{1,0:T(8,128)} copy-done((f32[4096,256]{1,0:T(8,128)}, f32[4096,256]{1,0:T(8,128)S(1)}, u32[]{:S(2)}) %copy-start.1) | copy-done | bytes 4194328
  36.7 17.7 %fusion.1 = f32[256,2048]{1,0:T(8,128)} fusion(f32[2048,2048]{1,0:T(8,128)} %param.3, f32[4096,256]{1,0:T(8,128)S(1)} %constant_dynamic-update-slice_fusion, s32[]{:T(128)S(6)} %select_n.14), kind=kOutput, calls=%fused_computation.2 | convolution fusion | flops 12884901888 | bytes 20971524 | tf_op jit(solution)/shard_map/dot_general | solution.py:15
  54.4 0.0 all-reduce.2.cloned.1.call-update
  54.4 104.5 %all-reduce.2.cloned.1.call-done = f32[256,2048]{1,0:T(8,128)} async-done(((f32[256,2048]{1,0:T(8,128)}), f32[256,2048]{1,0:T(8,128)}) %all-reduce.2.cloned.1.call-update) | async-done | bytes 2097168 | tf_op jit(solution)/shard_map/psum | solution.py:18
  158.9 0.0 copy-done
  158.9 0.0 copy-start.2
  158.9 5.3 %fusion.5 = f32[2048,256]{1,0:T(8,128)S(1)} fusion(f32[256,2048]{1,0:T(8,128)} %all-reduce.2.cloned.1.call-done, f32[256,256]{1,0:T(8,128)S(1)} %copy-done), kind=kOutput, calls=%fused_computation.14 | convolution fusion | flops 1610612736 | bytes 4456448 | tf_op jit(solution)/shard_map/dot_general | solution.py:19
  164.2 0.0 copy-done.2
  164.3 18.5 %convolution_subtract_fusion = f32[2048,2048]{1,0:T(8,128)} fusion(f32[2048,2048]{1,0:T(8,128)} %param.3, f32[2048,256]{1,0:T(8,128)S(1)} %fusion.5, f32[4096,256]{1,0:T(8,128)S(1)} %copy-done.2, s32[]{:T(128)S(6)} %select_n.14), kind=kOutput, calls=%fused_computation | convolution fusion | flops 12889096192 | bytes 37748740 | tf_op jit(solution)/shard_map/dot_general | solution.py:20
  (7 shorter events, 0.3 us)
Async XLA Ops:
  6.5 152.4 %copy-start = (f32[256,256]{1,0:T(8,128)S(1)}, f32[256,256]{1,0:T(8,128)}, u32[]{:S(2)}) copy-start(f32[256,256]{1,0:T(8,128)} %param.5) | copy-start | bytes 786436
  6.5 28.1 %copy-start.3 = (f32[512,256]{1,0:T(8,128)S(1)}, f32[512,256]{1,0:T(8,128)}, u32[]{:S(2)}) copy-start(f32[512,256]{1,0:T(8,128)} %param.4) | copy-start | bytes 1572868
  6.5 152.4 %all-reduce.2.cloned.1.call-start = ((), (), s32[]{:S(2)}) async-start(), calls=%async_computation | async-start | bytes 4194304 | tf_op jit(solution)/shard_map/psum | solution.py:18
  6.5 9.5 %collective-permute-start = (f32[512,256]{1,0:T(8,128)}, f32[512,256]{1,0:T(8,128)S(1)}, u32[]{:S(2)}, u32[]{:S(2)}) collective-permute-start(f32[512,256]{1,0:T(8,128)} %param.4), channel_id=1, source_target_pairs={{0,1},{1,2},{2,3},{3,0},{4,5},{5,6},{6,7},{7,4},{8,9},{9,10},{10,1... | collective-permute-start | bytes 1572872 | tf_op jit(solution)/shard_map/ppermute | solution.py:11
  16.1 8.6 %collective-permute-start.1 = (f32[512,256]{1,0:T(8,128)S(1)}, f32[512,256]{1,0:T(8,128)S(1)}, u32[]{:S(2)}, u32[]{:S(2)}) collective-permute-start(f32[512,256]{1,0:T(8,128)S(1)} %collective-permute-done), channel_id=1, source_target_pairs={{0,1},{1,2},{2,3},{3,0},{4,5},{5,6},{6,7},{7,4},{8,9},{9,10},{10,1... | collective-permute-start | bytes 1572872 | tf_op jit(solution)/shard_map/ppermute | solution.py:11
  24.7 8.6 %collective-permute-start.2 = (f32[512,256]{1,0:T(8,128)S(1)}, f32[512,256]{1,0:T(8,128)S(1)}, u32[]{:S(2)}, u32[]{:S(2)}) collective-permute-start(f32[512,256]{1,0:T(8,128)S(1)} %collective-permute-done.1), channel_id=1, source_target_pairs={{0,1},{1,2},{2,3},{3,0},{4,5},{5,6},{6,7},{7,4},{8,9},{9,10},{10,1... | collective-permute-start | bytes 1572872 | tf_op jit(solution)/shard_map/ppermute | solution.py:11
  34.7 2.0 %copy-start.1 = (f32[4096,256]{1,0:T(8,128)}, f32[4096,256]{1,0:T(8,128)S(1)}, u32[]{:S(2)}) copy-start(f32[4096,256]{1,0:T(8,128)S(1)} %constant_dynamic-update-slice_fusion) | copy-start | bytes 12582916
  158.9 5.3 %copy-start.2 = (f32[4096,256]{1,0:T(8,128)S(1)}, f32[4096,256]{1,0:T(8,128)}, u32[]{:S(2)}) copy-start(f32[4096,256]{1,0:T(8,128)} %copy-done.1) | copy-start | bytes 12582916
Sparse Core Ops, SparseCore 0:
  54.6 104.3 all-reduce.1
